TPU v7x, 32 devices: a whole 2x2x4 slice. The times are simulated.
32 devices in a mesh: mem: 4 (over y, core), lat: 4 (over z), lon: 2 (over x).
Axes of the slice: x: 2, y: 2, z: 4, core: 2. Of those that a mesh axis runs over, the one named last changes fastest.
Arguments:
- fields: bfloat16 [4, 2, 96, 96, 512], P('mem', None, 'lat', 'lon'), may hold values from -6 to 6
- region: int32 [96, 96], P('lat', 'lon'), may hold values from 0 to 2
- gain_attn: float32 [512], replicated, may hold values from 0.1 to 1.9
- w_qkv: bfloat16 [512, 1536], P(None, ('mem', 'lat', 'lon')), may hold values from -1 to 1
- w_proj: bfloat16 [512, 512], P(None, ('mem', 'lat', 'lon')), may hold values from -0.25 to 0.25
- gain_mlp: float32 [512], replicated, may hold values from 0.1 to 1.9
- w_up: bfloat16 [512, 2048], P(None, ('mem', 'lat', 'lon')), may hold values from -0.25 to 0.25
- w_down: bfloat16 [2048, 512], P(None, ('mem', 'lat', 'lon')), may hold values from -0.125 to 0.125
Outputs:
- updated: bfloat16 [4, 2, 96, 96, 512], P('mem', None, 'lat', 'lon')
All inputs are finite; a program needn't handle non-finite values.
Results may differ from a plain program's by a relative error of at most 0.011.
Values may be sent and summed in bfloat16 or wider, within the bound.
A program may use at most 192 MiB of HBM per device.

v0:
```python
import jax
import jax.numpy as jnp
from jax import lax
from jax.sharding import PartitionSpec as P

HEADS = 16
HDIM = 32
WLAT = 6
WLON = 12
SH = 3
SL = 6
eps = 1e-05


def shifted_2(block, axis, distance):
    devices = range(lax.axis_size(axis))
    route = [((i - distance) % len(devices), i) for i in devices]
    return lax.ppermute(block, axis, route)


def layer_norm(values, gain_vec):
    values = values.astype(jnp.float32)
    average = jnp.mean(values, axis=-1, keepdims=True)
    centred = values - average
    variance = jnp.mean(centred * centred, axis=-1, keepdims=True)
    return (centred * lax.rsqrt(variance + eps) * gain_vec).astype(jnp.bfloat16)


def attend(qkv_all, region_ids, north_side, height):
    levels, row_count, col_count, width3 = qkv_all.shape
    width = width3 // 3
    band_count = row_count // height
    win_count = col_count // WLON
    win_tok = levels * height * WLON
    windowed = qkv_all.reshape(levels, band_count, height, win_count, WLON, width3)
    windowed = windowed.transpose(1, 3, 0, 2, 4, 5).reshape(
        band_count * win_count, win_tok, 3, HEADS, width // HEADS
    )
    ids_full = jnp.broadcast_to(region_ids[None], (levels, row_count, col_count))
    ids_full = ids_full.reshape(levels, band_count, height, win_count, WLON).transpose(
        1, 3, 0, 2, 4
    )
    ids_full = ids_full.reshape(band_count * win_count, win_tok)
    north_full = jnp.broadcast_to(north_side[None, :, None], (levels, row_count, col_count))
    north_full = north_full.reshape(levels, band_count, height, win_count, WLON).transpose(
        1, 3, 0, 2, 4
    )
    north_full = north_full.reshape(band_count * win_count, win_tok)
    scores = jnp.einsum(
        "wqhd,wkhd->whqk", windowed[:, :, 0], windowed[:, :, 1], preferred_element_type=jnp.float32
    )
    scores = scores * (1.0 / HDIM**0.5)
    allow = (ids_full[:, :, None] == ids_full[:, None, :]) & (
        north_full[:, :, None] == north_full[:, None, :]
    )
    scores = jnp.where(allow[:, None], scores, -1000000000.0)
    attn_probs = jax.nn.softmax(scores, axis=-1).astype(jnp.bfloat16)
    mixed_heads = jnp.einsum(
        "whqk,wkhd->wqhd", attn_probs, windowed[:, :, 2], preferred_element_type=jnp.float32
    )
    mixed_heads = mixed_heads.astype(jnp.bfloat16).reshape(
        band_count, win_count, levels, height, WLON, width
    )
    return mixed_heads.transpose(2, 0, 3, 1, 4, 5).reshape(levels, row_count, col_count, width)


def body(fields, region, gain_attn, w_qkv, w_proj, gain_mlp, w_up, w_down):
    member = fields[0]
    levels, clat, clon, width = member.shape
    normed = layer_norm(member, gain_attn)
    region_ids = region.astype(jnp.bfloat16)
    lat_pos = lax.axis_index("lat")
    nlat_all = clat * lax.axis_size("lat")
    row_ids = jnp.arange(clat, dtype=jnp.int32)
    north_side = (lat_pos * clat + SH + row_ids) % nlat_all < SH
    arrived, arrived_ids = shifted_2((normed[:, :SH], region_ids[:SH]), "lat", -1)
    lat_band = jnp.concatenate([normed[:, SH:], arrived], axis=1)
    band_ids = jnp.concatenate([region_ids[SH:], arrived_ids], axis=0)
    strip, strip_ids = shifted_2((lat_band[:, :, :SL], band_ids[:, :SL]), "lon", -1)
    shifted = jnp.concatenate([lat_band[:, :, SL:], strip], axis=2)
    shifted_ids = jnp.concatenate([band_ids[:, SL:], strip_ids], axis=1)
    tok_rows = shifted.reshape(-1, width)
    qkv_all = (
        jnp.dot(
            tok_rows,
            lax.all_gather(w_qkv, ("mem", "lat", "lon"), axis=1, tiled=True),
            preferred_element_type=jnp.float32,
        )
        .astype(jnp.bfloat16)
        .reshape(levels, clat, clon, 3 * width)
    )
    mixed_heads = attend(qkv_all, shifted_ids, north_side, WLAT)
    proj_tok_rows = mixed_heads.reshape(-1, width)
    attn_out = (
        jnp.dot(
            proj_tok_rows,
            lax.all_gather(w_proj, ("mem", "lat", "lon"), axis=1, tiled=True),
            preferred_element_type=jnp.float32,
        )
        .astype(jnp.bfloat16)
        .reshape(levels, clat, clon, width)
    )
    arrived_cols = shifted_2(attn_out[:, :, clon - SL :], "lon", 1)
    attn_out = jnp.concatenate([arrived_cols, attn_out[:, :, : clon - SL]], axis=2)
    arrived_rows = shifted_2(attn_out[:, clat - SH :], "lat", 1)
    attn_out = jnp.concatenate([arrived_rows, attn_out[:, : clat - SH]], axis=1)
    resid = (member.astype(jnp.float32) + attn_out.astype(jnp.float32)).astype(jnp.bfloat16)
    normed2 = layer_norm(resid, gain_mlp).reshape(-1, width)
    pre_act = jnp.dot(
        normed2,
        lax.all_gather(w_up, ("mem", "lat", "lon"), axis=1, tiled=True),
        preferred_element_type=jnp.float32,
    )
    hidden = jax.nn.gelu(pre_act, approximate=False).astype(jnp.bfloat16)
    delta = jnp.dot(
        hidden,
        lax.all_gather(w_down, ("mem", "lat", "lon"), axis=1, tiled=True),
        preferred_element_type=jnp.float32,
    ).reshape(levels, clat, clon, width)
    updated = (resid.astype(jnp.float32) + delta).astype(jnp.bfloat16)
    return updated[None]


def solution(mesh):
    in_specs = (
        P("mem", None, "lat", "lon", None),
        P("lat", "lon"),
        P(),
        P(None, ("mem", "lat", "lon")),
        P(None, ("mem", "lat", "lon")),
        P(),
        P(None, ("mem", "lat", "lon")),
        P(None, ("mem", "lat", "lon")),
    )
    out_specs = P("mem", None, "lat", "lon", None)
    return jax.shard_map(body, mesh=mesh, in_specs=in_specs, out_specs=out_specs, check_vma=False)
```

profile of v0, /device:TPU:0, one launch (start us, length us, event | category | flops | bytes accessed | tf_op | source)
XLA Modules:
  0.0 395.8 jit_solution(3137256965465653519)
XLA Ops:
  9.4 2.7 fusion.27
  14.5 5.1 %collective-permute-start = (bf16[2,3,48,512]{3,2,1,0:T(8,128)(2,1)S(1)}, bf16[2,3,48,512]{3,2,1,0:T(8,128)(2,1)S(1)}, u32[]{:S(2)}, u32[]{:S(2)}) collective-permute-start(bf16[2,3,48,512]{3,2,1,0:T(8,128)(2,1)S(1)} %slice.61), channel_id=1, source_target_pairs={{2,0},{4,2},{6,4},{0,6},{3,1},{5,3},{7,5},{1,7},{10,8},{12,10},{14... | collective-permute-start | bytes 884744 | tf_op jit(solution)/shard_map/ppermute | solution.py:18
  20.2 76.2 %all_gather.13 = bf16[512,512]{0,1:T(8,128)(2,1)} all-gather(bf16[512,16]{0,1:T(8,128)(2,1)S(1)} %copy-done.6), channel_id=1, replica_groups=mesh['mem'=4,'lat'=4,'lon'=2] {'mem','lat','lon'}, dimensions={1}, use_global_device_ids=true | all-gather | bytes 540672 | tf_op jit(solution)/shard_map/all_gather | solution.py:97
  98.7 3.7 collective-permute-done.3
  104.8 5.8 %collective-permute-done.1 = bf16[2,24,6,512]{3,2,1,0:T(8,128)(2,1)S(1)} collective-permute-done((bf16[2,24,6,512]{3,2,1,0:T(8,128)(2,1)S(1)}, bf16[2,24,6,512]{3,2,1,0:T(8,128)(2,1)S(1)}, u32[]{:S(2)}, u32[]{:S(2)}) %collective-permute-start.1) | collective-permute-done | bytes 294944 | tf_op jit(solution)/shard_map/ppermute | solution.py:18
  111.0 7.3 %convolution_convert_fusion = bf16[2304,1536]{1,0:T(8,128)(2,1)} fusion(bf16[2304,512]{1,0:T(8,128)(2,1)S(1)} %bitcast.91, bf16[512,1536]{0,1:T(8,128)(2,1)} %all-gather.4.cloned.1.call-done), kind=kOutput, calls=%fused_computation.29 | convolution fusion | flops 3627417600 | bytes 11010048 | tf_op jit(solution)/shard_map/dot_general | solution.py:84
  118.3 11.4 %reshape_reshape.6 = bf16[2,4,6,4,12,1536]{5,4,3,2,1,0:T(8,128)(2,1)} reshape(bf16[2304,1536]{1,0:T(8,128)(2,1)} %convolution_convert_fusion) | data formatting | bytes 14155776 | tf_op jit(solution)/shard_map/reshape;reshape | solution.py:35
  129.7 12.0 %copy.11 = bf16[4,4,2,6,12,1536]{5,1,0,4,3,2:T(4,128)(2,1)} copy(bf16[4,4,2,6,12,1536]{5,4,1,3,0,2:T(8,128)(2,1)} %bitcast.84) | data formatting | bytes 14155776 | tf_op jit(solution)/shard_map/transpose | solution.py:36
  141.6 32.5 %reshape.120 = bf16[16,144,3,16,32]{4,3,2,0,1:T(8,128)(2,1)} reshape(bf16[4,4,2,6,12,1536]{5,1,0,4,3,2:T(4,128)(2,1)} %copy.11) | data formatting | bytes 14155776 | tf_op jit(solution)/shard_map/reshape | solution.py:36
  174.1 24.0 %fusion.88 = (bf16[16,144,1,16,32]{4,3,2,0,1:T(8,128)(2,1)}, bf16[16,144,1,16,32]{4,3,2,0,1:T(8,128)(2,1)}, bf16[16,144,1,16,32]{4,3,2,0,1:T(8,128)(2,1)}) fusion(bf16[16,144,3,16,32]{4,3,2,0,1:T(8,128)(2,1)} %reshape.120), kind=kLoop, calls=%fused_computation.115 | loop fusion | bytes 14155776 | tf_op jit(solution)/shard_map/slice | solution.py:59
  198.1 12.3 %copy.21 = bf16[16,144,1,16,32]{1,4,3,0,2:T(8,128)(2,1)} copy(bf16[16,144,1,16,32]{4,3,2,0,1:T(8,128)(2,1)} %get-tuple-element.6) | data formatting | bytes 4718592
  210.4 12.4 %copy.22 = bf16[16,144,1,16,32]{1,4,3,0,2:T(8,128)(2,1)} copy(bf16[16,144,1,16,32]{4,3,2,0,1:T(8,128)(2,1)} %get-tuple-element.7) | data formatting | bytes 4718592
  222.8 12.3 %copy.20 = bf16[16,144,1,16,32]{1,4,3,0,2:T(8,128)(2,1)} copy(bf16[16,144,1,16,32]{4,3,2,0,1:T(8,128)(2,1)} %get-tuple-element.5) | data formatting | bytes 4718592
  235.1 19.9 %fusion.89 = (f32[16,16,144]{2,1,0:T(8,128)S(1)}, f32[16,16,144,144]{2,3,1,0:T(8,128)}) fusion(pred[16,144,144]{1,2,0:T(8,128)(4,1)S(1)} %compare_and_fusion, bf16[16,144,1,16,32]{1,4,3,0,2:T(8,128)(2,1)} %copy.22, bf16[16,144,1,16,32]{1,4,3,0,2:T(8,128)(2,1)} %copy.21), kind=kOutput, calls=%fused_computation.116 | convolution fusion | flops 360972416 | bytes 26431488 | tf_op jit(solution)/shard_map/sub | solution.py:57
  255.0 16.4 %convert_bitcast_fusion = bf16[16,144,16,32]{1,3,2,0:T(8,128)(2,1)} fusion(f32[16,16,144,144]{2,3,1,0:T(8,128)} %get-tuple-element.9, f32[16,16,144]{2,1,0:T(8,128)S(1)} %get-tuple-element.8, bf16[16,144,1,16,32]{1,4,3,0,2:T(8,128)(2,1)} %copy.20), kind=kOutput, calls=%fused_computation.58 | convolution fusion | flops 351535104 | bytes 26099712 | tf_op jit(solution)/shard_map/whqk,wkhd->wqhd/dot_general | solution.py:58
  271.4 11.5 %copy.17 = bf16[16,144,16,32]{3,2,0,1:T(8,128)(2,1)} copy(bf16[16,144,16,32]{1,3,2,0:T(8,128)(2,1)} %convert_bitcast_fusion) | data formatting | bytes 4718592 | tf_op jit(solution)/shard_map/convert_element_type | solution.py:61
  282.9 13.0 %reshape.121 = bf16[4,4,2,6,12,512]{5,1,0,4,3,2:T(4,128)(2,1)} reshape(bf16[16,144,16,32]{3,2,0,1:T(8,128)(2,1)} %copy.17) | data formatting | bytes 4718592 | tf_op jit(solution)/shard_map/reshape | solution.py:61
  295.9 3.9 copy.18
  301.9 3.2 convolution_convert_fusion.1
  305.3 7.7 %collective-permute-done.4 = bf16[2,24,6,512]{3,2,1,0:T(8,128)(2,1)S(1)} collective-permute-done((bf16[2,24,6,512]{3,2,1,0:T(8,128)(2,1)S(1)}, bf16[2,24,6,512]{3,2,1,0:T(8,128)(2,1)S(1)}, u32[]{:S(2)}, u32[]{:S(2)}) %collective-permute-start.4) | collective-permute-done | bytes 294944 | tf_op jit(solution)/shard_map/ppermute | solution.py:18
  313.2 2.8 pad_maximum_fusion.1
  316.0 7.3 %collective-permute-done.5 = bf16[2,3,48,512]{3,2,1,0:T(8,128)(2,1)S(1)} collective-permute-done((bf16[2,3,48,512]{3,2,1,0:T(8,128)(2,1)S(1)}, bf16[2,3,48,512]{3,2,1,0:T(8,128)(2,1)S(1)}, u32[]{:S(2)}, u32[]{:S(2)}) %collective-permute-start.5) | collective-permute-done | bytes 294944 | tf_op jit(solution)/shard_map/ppermute | solution.py:18
  331.0 47.1 %fusion.110 = bf16[2304,2048]{1,0:T(8,128)(2,1)} fusion(bf16[512,2048]{0,1:T(8,128)(2,1)} %all-gather.6.cloned.1.call-done, bf16[2304,512]{1,0:T(8,128)(2,1)} %fusion.24, f32[512]{0:T(512)S(1)} %copy-done.9, f32[2304]{0:T(1024)S(1)} %rsqrt.21, f32[2304]{0:T(1024)S(1)} %div.27), kind=kOutput, calls=%fused_computation.8.clone.clone.1 | convolution fusion | flops 5144444928 | bytes 13914112 | tf_op jit(solution)/shard_map/dot_general | solution.py:109
  378.0 8.5 %fusion.18 = f32[2304,512]{1,0:T(8,128)S(1)} fusion(bf16[2048,512]{0,1:T(8,128)(2,1)} %all-gather.8.cloned.1.call-done, bf16[2304,2048]{1,0:T(8,128)(2,1)} %fusion.110), kind=kOutput, calls=%fused_computation.30 | convolution fusion | flops 4831838208 | bytes 16252928 | tf_op jit(solution)/shard_map/dot_general | solution.py:115
  (71 shorter events, 23.3 us)
Async XLA Ops:
  6.5 5.6 %copy-start = (bf16[1,2,24,48,512]{4,3,2,1,0:T(8,128)(2,1)S(1)}, bf16[1,2,24,48,512]{4,3,2,1,0:T(8,128)(2,1)}, u32[]{:S(2)}) copy-start(bf16[1,2,24,48,512]{4,3,2,1,0:T(8,128)(2,1)} %param.8) | copy-start | bytes 7077892
  6.5 5.6 %copy-start.8 = (f32[512]{0:T(512)S(1)}, f32[512]{0:T(512)}, u32[]{:S(2)}) copy-start(f32[512]{0:T(512)} %param.10) | copy-start | bytes 6148
  6.5 104.4 %all-gather.4.cloned.1.call-start = ((), (), s32[]{:S(2)}) async-start(), calls=%async_computation | async-start | bytes 1622016 | tf_op jit(solution)/shard_map/all_gather | solution.py:86
  7.3 12.4 %copy-start.7 = (s32[24,48]{1,0:T(8,128)S(1)}, s32[24,48]{1,0:T(8,128)}, u32[]{:S(2)}) copy-start(s32[24,48]{1,0:T(8,128)} %param.9) | copy-start | bytes 13828
  7.3 13.0 %copy-start.6 = (bf16[512,16]{0,1:T(8,128)(2,1)S(1)}, bf16[512,16]{0,1:T(8,128)(2,1)}, u32[]{:S(2)}) copy-start(bf16[512,16]{0,1:T(8,128)(2,1)} %param.12) | copy-start | bytes 49156
  7.3 323.7 %all-gather.6.cloned.1.call-start = ((), (), s32[]{:S(2)}) async-start(), calls=%async_computation.1 | async-start | bytes 2162688 | tf_op jit(solution)/shard_map/all_gather | solution.py:111
  13.1 1.4 copy-start.5
  14.5 88.2 %collective-permute-start = (bf16[2,3,48,512]{3,2,1,0:T(8,128)(2,1)S(1)}, bf16[2,3,48,512]{3,2,1,0:T(8,128)(2,1)S(1)}, u32[]{:S(2)}, u32[]{:S(2)}) collective-permute-start(bf16[2,3,48,512]{3,2,1,0:T(8,128)(2,1)S(1)} %slice.61), channel_id=1, source_target_pairs={{2,0},{4,2},{6,4},{0,6},{3,1},{5,3},{7,5},{1,7},{10,8},{12,10},{14... | collective-permute-start | bytes 884744 | tf_op jit(solution)/shard_map/ppermute | solution.py:18
  19.7 78.8 %collective-permute-start.2 = (bf16[3,48]{1,0:T(4,128)(2,1)S(1)}, bf16[3,48]{1,0:T(4,128)(2,1)S(1)}, u32[]{:S(2)}, u32[]{:S(2)}) collective-permute-start(bf16[3,48]{1,0:T(4,128)(2,1)S(1)} %slice.66), channel_id=1, source_target_pairs={{2,0},{4,2},{6,4},{0,6},{3,1},{5,3},{7,5},{1,7},{10,8},{12,10},{14... | collective-permute-start | bytes 872 | tf_op jit(solution)/shard_map/ppermute | solution.py:18
  20.2 357.8 %all-gather.8.cloned.1.call-start = ((), (), s32[]{:S(2)}) async-start(), calls=%async_computation.2 | async-start | bytes 2162688 | tf_op jit(solution)/shard_map/all_gather | solution.py:117
  98.5 3.9 collective-permute-start.3
  102.8 7.8 %collective-permute-start.1 = (bf16[2,24,6,512]{3,2,1,0:T(8,128)(2,1)S(1)}, bf16[2,24,6,512]{3,2,1,0:T(8,128)(2,1)S(1)}, u32[]{:S(2)}, u32[]{:S(2)}) collective-permute-start(bf16[2,24,6,512]{3,2,1,0:T(8,128)(2,1)S(1)} %pad_maximum_fusion.2), channel_id=1, source_target_pairs={{1,0},{0,1},{3,2},{2,3},{5,4},{4,5},{7,6},{6,7},{9,8},{8,9},{11,10... | collective-permute-start | bytes 884744 | tf_op jit(solution)/shard_map/ppermute | solution.py:18
  305.0 8.0 %copy-start.4 = (bf16[2304,512]{1,0:T(8,128)(2,1)}, bf16[2304,512]{1,0:T(8,128)(2,1)S(1)}, u32[]{:S(2)}) copy-start(bf16[2304,512]{1,0:T(8,128)(2,1)S(1)} %convolution_convert_fusion.1) | copy-start | bytes 7077892
  305.1 18.2 %copy-start.1 = (bf16[1,2,24,48,512]{4,3,2,1,0:T(8,128)(2,1)S(1)}, bf16[1,2,24,48,512]{4,3,2,1,0:T(8,128)(2,1)}, u32[]{:S(2)}) copy-start(bf16[1,2,24,48,512]{4,3,2,1,0:T(8,128)(2,1)} %param.8) | copy-start | bytes 7077892
  305.2 7.8 %collective-permute-start.4 = (bf16[2,24,6,512]{3,2,1,0:T(8,128)(2,1)S(1)}, bf16[2,24,6,512]{3,2,1,0:T(8,128)(2,1)S(1)}, u32[]{:S(2)}, u32[]{:S(2)}) collective-permute-start(bf16[2,24,6,512]{3,2,1,0:T(8,128)(2,1)S(1)} %slice.71), channel_id=1, source_target_pairs={{1,0},{0,1},{3,2},{2,3},{5,4},{4,5},{7,6},{6,7},{9,8},{8,9},{11,10... | collective-permute-start | bytes 884744 | tf_op jit(solution)/shard_map/ppermute | solution.py:18
  313.1 10.2 %collective-permute-start.5 = (bf16[2,3,48,512]{3,2,1,0:T(8,128)(2,1)S(1)}, bf16[2,3,48,512]{3,2,1,0:T(8,128)(2,1)S(1)}, u32[]{:S(2)}, u32[]{:S(2)}) collective-permute-start(bf16[2,3,48,512]{3,2,1,0:T(8,128)(2,1)S(1)} %pad_maximum_fusion.3), channel_id=1, source_target_pairs={{6,0},{0,2},{2,4},{4,6},{7,1},{1,3},{3,5},{5,7},{14,8},{8,10},{10,... | collective-permute-start | bytes 884744 | tf_op jit(solution)/shard_map/ppermute | solution.py:18
  316.0 7.3 %copy-start.2 = (bf16[2,21,48,512]{3,2,1,0:T(8,128)(2,1)}, bf16[2,21,48,512]{3,2,1,0:T(8,128)(2,1)S(1)}, u32[]{:S(2)}) copy-start(bf16[2,21,48,512]{3,2,1,0:T(8,128)(2,1)S(1)} %pad_maximum_fusion.1) | copy-start | bytes 6193156
  328.7 2.3 copy-start.9
  378.0 8.5 %copy-start.3 = (bf16[2,21,48,512]{3,2,1,0:T(8,128)(2,1)S(1)}, bf16[2,21,48,512]{3,2,1,0:T(8,128)(2,1)}, u32[]{:S(2)}) copy-start(bf16[2,21,48,512]{3,2,1,0:T(8,128)(2,1)} %copy-done.2) | copy-start | bytes 6193156
Sparse Core Ops, SparseCore 0:
  10.3 60.3 all-gather.3
  73.7 56.7 all-gather.5
  313.3 57.8 all-gather.7
where the time goes:
time: 402 us; the launch traced here: 396 us
  local copies, waits for them, and re-layouts  151 us (38%)
  matrix products  102 us (25%)
  blocking collectives  76.2 us (19%)
  waiting for transfers between devices  25.3 us (6%)
  other arithmetic  21.1 us (5%)
  between operations  13.7 us (3%)
  starting transfers between devices  6.03 us (2%)
    all_gather x1, blocking collectives, body(): lax.all_gather(w_proj, ('mem', 'lat', 'lon'), axis=1, tiled=True)  76.2 us
    dot_general x1, matrix products, body(): jnp.dot(normed2, lax.all_gather(w_up, ('mem', 'lat', 'lon'), axis=1, tile...  47.1 us
    unnamed x23, local copies, waits for them, and re-layouts  38.4 us
    reshape x1, local copies, waits for them, and re-layouts, attend(): windowed.transpose(1, 3, 0, 2, 4, 5)  32.5 us
    ppermute x6, waiting for transfers between devices, shifted_2(): return lax.ppermute(block, axis, route)  24.5 us
    slice x1, local copies, waits for them, and re-layouts, attend(): windowed[:, :, 2]  24 us
    sub x1, matrix products, attend(): attn_probs = jax.nn.softmax(scores, axis=-1).astype(jnp.bfloat16)  19.9 us
    dot_general x1, matrix products, attend(): jnp.einsum('whqk,wkhd->wqhd', attn_probs, windowed[:, :, 2], preferred_el...  16.4 us
  transfers between devices with their start and end apart: 9, of which 4 were waited for; matrix products, arithmetic and copies ran while one was open for 66% of the time, Pallas kernels for 0%

commit v1 on v0

--- a/solution.py
+++ b/solution.py
@@ -10,6 +10,33 @@
 SH = 3
 SL = 6
 eps = 1e-05
+
+
+def wait_sheet(z, at_axis):
+    small = list(z.shape[1:])
+    small[at_axis] *= z.shape[0]
+    top = jnp.moveaxis(z, 0, at_axis).reshape(small)
+    return top
+
+
+def answer_column(raw, comm_axis):
+    high, seen_now = (lax.axis_size(comm_axis), lax.axis_index(comm_axis))
+    next_value, frame_out = (raw[None], 1)
+    while frame_out < high:
+        v_now = lax.ppermute(
+            next_value, comm_axis, tuple(((no, no ^ frame_out) for no in range(high)))
+        )
+        known = seen_now & frame_out == 0
+        next_value = jnp.concatenate(
+            [jnp.where(known, next_value, v_now), jnp.where(known, v_now, next_value)]
+        )
+        frame_out *= 2
+    return next_value
+
+
+def replace_screen(mine_x, patch, on_dim):
+    vec_out = wait_sheet(answer_column(mine_x, patch), on_dim)
+    return vec_out
 
 
 def shifted_2(block, axis, distance):
@@ -94,7 +121,7 @@
     attn_out = (
         jnp.dot(
             proj_tok_rows,
-            lax.all_gather(w_proj, ("mem", "lat", "lon"), axis=1, tiled=True),
+            replace_screen(w_proj, ("mem", "lat", "lon"), 1),
             preferred_element_type=jnp.float32,
         )
         .astype(jnp.bfloat16)

time: 402 us -> 365 us (0.908)
  blocking collectives: 76.2 us -> 0 us
  waiting for transfers between devices: 25.3 us -> 53.5 us
  starting transfers between devices: 6.03 us -> 16 us
    all_gather x1 -> x0, blocking collectives: 76.2 us -> none  [body(): lax.all_gather(w_proj, ('mem', 'lat', 'lon'), axis=1, tiled=True)]
    all_gather x1, waiting for transfers between devices: 0.02 us -> 17.7 us  [body(): lax.all_gather(w_qkv, ('mem', 'lat', 'lon'), axis=1, tiled=True)]
    ppermute x0 -> x5, waiting for transfers between devices: none -> 7.73 us  [answer_column(): lax.ppermute(next_value, comm_axis, tuple(((no, no ^ frame_out) for no in...]
    ppermute x0 -> x5, starting transfers between devices: none -> 7.72 us  [answer_column(): lax.ppermute(next_value, comm_axis, tuple(((no, no ^ frame_out) for no in...]
  transfers between devices with their start and end apart: 9 -> 14, of which waited for: 4 -> 9; matrix products, arithmetic and copies ran while one was open for 66% -> 73% of each run, Pallas kernels for 0% -> 0%
where the time goes in v1:
time: 365 us; the launch traced here: 359 us
  local copies, waits for them, and re-layouts  151 us (41%)
  matrix products  102 us (28%)
  waiting for transfers between devices  53.5 us (15%)
  other arithmetic  22.1 us (6%)
  starting transfers between devices  16 us (4%)
  between operations  13.7 us (4%)
    dot_general x1, matrix products, body(): jnp.dot(normed2, lax.all_gather(w_up, ('mem', 'lat', 'lon'), axis=1, tile...  47.1 us
    unnamed x23, local copies, waits for them, and re-layouts  38.4 us
    reshape x1, local copies, waits for them, and re-layouts, attend(): windowed.transpose(1, 3, 0, 2, 4, 5)  32.5 us
    ppermute x6, waiting for transfers between devices, shifted_2(): return lax.ppermute(block, axis, route)  27.3 us
    slice x1, local copies, waits for them, and re-layouts, attend(): windowed[:, :, 2]  24 us
    sub x1, matrix products, attend(): attn_probs = jax.nn.softmax(scores, axis=-1).astype(jnp.bfloat16)  19.9 us
    all_gather x1, waiting for transfers between devices, body(): lax.all_gather(w_qkv, ('mem', 'lat', 'lon'), axis=1, tiled=True)  17.7 us
    dot_general x1, matrix products, attend(): jnp.einsum('whqk,wkhd->wqhd', attn_probs, windowed[:, :, 2], preferred_el...  16.5 us
  transfers between devices with their start and end apart: 14, of which 9 were waited for; matrix products, arithmetic and copies ran while one was open for 73% of the time, Pallas kernels for 0%

profile of v1, /device:TPU:0, one launch (start us, length us, event | category | flops | bytes accessed | tf_op | source)
XLA Modules:
  0.0 358.8 jit_solution(15074551082594106125)
XLA Ops:
  7.3 3.0 collective-permute-start.4
  17.5 3.7 %collective-permute-start = (bf16[2,3,48,512]{3,2,1,0:T(8,128)(2,1)S(1)}, bf16[2,3,48,512]{3,2,1,0:T(8,128)(2,1)S(1)}, u32[]{:S(2)}, u32[]{:S(2)}) collective-permute-start(bf16[2,3,48,512]{3,2,1,0:T(8,128)(2,1)S(1)} %slice.61), channel_id=1, source_target_pairs={{2,0},{4,2},{6,4},{0,6},{3,1},{5,3},{7,5},{1,7},{10,8},{12,10},{14... | collective-permute-start | bytes 884744 | tf_op jit(solution)/shard_map/ppermute | solution.py:45
  23.8 4.5 %collective-permute-done.2 = bf16[3,48]{1,0:T(4,128)(2,1)S(1)} collective-permute-done((bf16[3,48]{1,0:T(4,128)(2,1)S(1)}, bf16[3,48]{1,0:T(4,128)(2,1)S(1)}, u32[]{:S(2)}, u32[]{:S(2)}) %collective-permute-start.2) | collective-permute-done | bytes 320 | tf_op jit(solution)/shard_map/ppermute | solution.py:45
  28.7 3.3 collective-permute-done.3
  43.6 5.1 %collective-permute-done.8 = bf16[16,512,16]{1,2,0:T(8,128)(2,1)S(1)} collective-permute-done((bf16[16,512,16]{1,2,0:T(8,128)(2,1)S(1)}, bf16[16,512,16]{1,2,0:T(8,128)(2,1)S(1)}, u32[]{:S(2)}, u32[]{:S(2)}) %collective-permute-start.8) | collective-permute-done | bytes 262176 | tf_op jit(solution)/shard_map/ppermute | solution.py:26
  52.8 17.7 %all-gather.4.cloned.1.call-done = bf16[512,1536]{0,1:T(8,128)(2,1)} async-done(((bf16[512,48]{0,1:T(8,128)(2,1)}), bf16[512,1536]{0,1:T(8,128)(2,1)}) %all-gather.4.cloned.1.call-update) | async-done | bytes 1572880 | tf_op jit(solution)/shard_map/all_gather | solution.py:113
  70.5 7.2 %convolution_convert_fusion = bf16[2304,1536]{1,0:T(8,128)(2,1)} fusion(bf16[2304,512]{1,0:T(8,128)(2,1)S(1)} %bitcast.97, bf16[512,1536]{0,1:T(8,128)(2,1)} %all-gather.4.cloned.1.call-done), kind=kOutput, calls=%fused_computation.29 | convolution fusion | flops 3627417600 | bytes 11010048 | tf_op jit(solution)/shard_map/dot_general | solution.py:111
  77.8 11.3 %reshape_reshape.6 = bf16[2,4,6,4,12,1536]{5,4,3,2,1,0:T(8,128)(2,1)} reshape(bf16[2304,1536]{1,0:T(8,128)(2,1)} %convolution_convert_fusion) | data formatting | bytes 14155776 | tf_op jit(solution)/shard_map/reshape;reshape | solution.py:62
  89.1 12.0 %copy.11 = bf16[4,4,2,6,12,1536]{5,1,0,4,3,2:T(4,128)(2,1)} copy(bf16[4,4,2,6,12,1536]{5,4,1,3,0,2:T(8,128)(2,1)} %bitcast.90) | data formatting | bytes 14155776 | tf_op jit(solution)/shard_map/transpose | solution.py:63
  101.1 32.5 %reshape.123 = bf16[16,144,3,16,32]{4,3,2,0,1:T(8,128)(2,1)} reshape(bf16[4,4,2,6,12,1536]{5,1,0,4,3,2:T(4,128)(2,1)} %copy.11) | data formatting | bytes 14155776 | tf_op jit(solution)/shard_map/reshape | solution.py:63
  133.6 24.0 %fusion.88 = (bf16[16,144,1,16,32]{4,3,2,0,1:T(8,128)(2,1)}, bf16[16,144,1,16,32]{4,3,2,0,1:T(8,128)(2,1)}, bf16[16,144,1,16,32]{4,3,2,0,1:T(8,128)(2,1)}) fusion(bf16[16,144,3,16,32]{4,3,2,0,1:T(8,128)(2,1)} %reshape.123), kind=kLoop, calls=%fused_computation.130 | loop fusion | bytes 14155776 | tf_op jit(solution)/shard_map/slice | solution.py:86
  157.6 12.3 %copy.21 = bf16[16,144,1,16,32]{1,4,3,0,2:T(8,128)(2,1)} copy(bf16[16,144,1,16,32]{4,3,2,0,1:T(8,128)(2,1)} %get-tuple-element.6) | data formatting | bytes 4718592
  169.9 12.4 %copy.22 = bf16[16,144,1,16,32]{1,4,3,0,2:T(8,128)(2,1)} copy(bf16[16,144,1,16,32]{4,3,2,0,1:T(8,128)(2,1)} %get-tuple-element.7) | data formatting | bytes 4718592
  182.3 12.3 %copy.20 = bf16[16,144,1,16,32]{1,4,3,0,2:T(8,128)(2,1)} copy(bf16[16,144,1,16,32]{4,3,2,0,1:T(8,128)(2,1)} %get-tuple-element.5) | data formatting | bytes 4718592
  194.6 19.9 %fusion.89 = (f32[16,16,144]{2,1,0:T(8,128)S(1)}, f32[16,16,144,144]{2,3,1,0:T(8,128)}) fusion(pred[16,144,144]{1,2,0:T(8,128)(4,1)S(1)} %compare_and_fusion, bf16[16,144,1,16,32]{1,4,3,0,2:T(8,128)(2,1)} %copy.22, bf16[16,144,1,16,32]{1,4,3,0,2:T(8,128)(2,1)} %copy.21), kind=kOutput, calls=%fused_computation.131 | convolution fusion | flops 360972416 | bytes 26431488 | tf_op jit(solution)/shard_map/sub | solution.py:84
  214.5 16.5 %convert_bitcast_fusion = bf16[16,144,16,32]{1,3,2,0:T(8,128)(2,1)} fusion(f32[16,16,144,144]{2,3,1,0:T(8,128)} %get-tuple-element.19, f32[16,16,144]{2,1,0:T(8,128)S(1)} %get-tuple-element.18, bf16[16,144,1,16,32]{1,4,3,0,2:T(8,128)(2,1)} %copy.20), kind=kOutput, calls=%fused_computation.58 | convolution fusion | flops 351535104 | bytes 26099712 | tf_op jit(solution)/shard_map/whqk,wkhd->wqhd/dot_general | solution.py:85
  231.0 11.5 %copy.17 = bf16[16,144,16,32]{3,2,0,1:T(8,128)(2,1)} copy(bf16[16,144,16,32]{1,3,2,0:T(8,128)(2,1)} %convert_bitcast_fusion) | data formatting | bytes 4718592 | tf_op jit(solution)/shard_map/convert_element_type | solution.py:88
  242.5 13.0 %reshape.124 = bf16[4,4,2,6,12,512]{5,1,0,4,3,2:T(4,128)(2,1)} reshape(bf16[16,144,16,32]{3,2,0,1:T(8,128)(2,1)} %copy.17) | data formatting | bytes 4718592 | tf_op jit(solution)/shard_map/reshape | solution.py:88
  255.4 3.9 %copy.18 = bf16[2,4,6,4,12,512]{5,4,3,2,1,0:T(8,128)(2,1)S(1)} copy(bf16[2,4,6,4,12,512]{5,3,1,4,2,0:T(4,128)(2,1)} %bitcast.94) | data formatting | bytes 4718592 | tf_op jit(solution)/shard_map/transpose | solution.py:91
  261.4 3.2 convolution_convert_fusion.1
  266.2 9.8 %collective-permute-done.9 = bf16[2,24,6,512]{3,2,1,0:T(8,128)(2,1)S(1)} collective-permute-done((bf16[2,24,6,512]{3,2,1,0:T(8,128)(2,1)S(1)}, bf16[2,24,6,512]{3,2,1,0:T(8,128)(2,1)S(1)}, u32[]{:S(2)}, u32[]{:S(2)}) %collective-permute-start.9) | collective-permute-done | bytes 294944 | tf_op jit(solution)/shard_map/ppermute | solution.py:45
  279.4 6.8 %collective-permute-done.10 = bf16[2,3,48,512]{3,2,1,0:T(8,128)(2,1)S(1)} collective-permute-done((bf16[2,3,48,512]{3,2,1,0:T(8,128)(2,1)S(1)}, bf16[2,3,48,512]{3,2,1,0:T(8,128)(2,1)S(1)}, u32[]{:S(2)}, u32[]{:S(2)}) %collective-permute-start.10) | collective-permute-done | bytes 294944 | tf_op jit(solution)/shard_map/ppermute | solution.py:45
  293.9 47.1 %fusion.110 = bf16[2304,2048]{1,0:T(8,128)(2,1)} fusion(bf16[512,2048]{0,1:T(8,128)(2,1)} %all-gather.6.cloned.1.call-done, bf16[2304,512]{1,0:T(8,128)(2,1)} %fusion.24, f32[512]{0:T(512)S(1)} %copy-done.9, f32[2304]{0:T(1024)S(1)} %rsqrt.21, f32[2304]{0:T(1024)S(1)} %div.27), kind=kOutput, calls=%fused_computation.8.clone.clone.1 | convolution fusion | flops 5144444928 | bytes 13914112 | tf_op jit(solution)/shard_map/dot_general | solution.py:136
  341.0 8.5 %fusion.18 = f32[2304,512]{1,0:T(8,128)S(1)} fusion(bf16[2048,512]{0,1:T(8,128)(2,1)} %all-gather.8.cloned.1.call-done, bf16[2304,2048]{1,0:T(8,128)(2,1)} %fusion.110), kind=kOutput, calls=%fused_computation.30 | convolution fusion | flops 4831838208 | bytes 16252928 | tf_op jit(solution)/shard_map/dot_general | solution.py:142
  (90 shorter events, 43.6 us)
Async XLA Ops:
  6.5 8.6 %copy-start = (bf16[1,2,24,48,512]{4,3,2,1,0:T(8,128)(2,1)S(1)}, bf16[1,2,24,48,512]{4,3,2,1,0:T(8,128)(2,1)}, u32[]{:S(2)}) copy-start(bf16[1,2,24,48,512]{4,3,2,1,0:T(8,128)(2,1)} %param.8) | copy-start | bytes 7077892
  6.5 8.6 %copy-start.8 = (f32[512]{0:T(512)S(1)}, f32[512]{0:T(512)}, u32[]{:S(2)}) copy-start(f32[512]{0:T(512)} %param.10) | copy-start | bytes 6148
  6.5 64.0 %all-gather.4.cloned.1.call-start = ((), (), s32[]{:S(2)}) async-start(), calls=%async_computation | async-start | bytes 1622016 | tf_op jit(solution)/shard_map/all_gather | solution.py:113
  7.3 286.7 %all-gather.6.cloned.1.call-start = ((), (), s32[]{:S(2)}) async-start(), calls=%async_computation.1 | async-start | bytes 2162688 | tf_op jit(solution)/shard_map/all_gather | solution.py:138
  7.3 13.9 %copy-start.7 = (s32[24,48]{1,0:T(8,128)S(1)}, s32[24,48]{1,0:T(8,128)}, u32[]{:S(2)}) copy-start(s32[24,48]{1,0:T(8,128)} %param.9) | copy-start | bytes 13828
  7.3 21.1 %collective-permute-start.4 = (bf16[1,512,16]{1,2,0:T(8,128)(2,1)}, bf16[1,512,16]{1,2,0:T(8,128)(2,1)S(1)}, u32[]{:S(2)}, u32[]{:S(2)}) collective-permute-start(bf16[1,512,16]{1,2,0:T(8,128)(2,1)} %bitcast.99), channel_id=1, source_target_pairs={{0,1},{1,0},{2,3},{3,2},{4,5},{5,4},{6,7},{7,6},{8,9},{9,8},{10,11... | collective-permute-start | bytes 49160 | tf_op jit(solution)/shard_map/ppermute | solution.py:26
  15.1 13.3 %copy-start.6 = (bf16[512,16]{0,1:T(8,128)(2,1)S(1)}, bf16[512,16]{0,1:T(8,128)(2,1)}, u32[]{:S(2)}) copy-start(bf16[512,16]{0,1:T(8,128)(2,1)} %param.12) | copy-start | bytes 49156
  16.1 1.4 copy-start.5
  17.5 23.4 %collective-permute-start = (bf16[2,3,48,512]{3,2,1,0:T(8,128)(2,1)S(1)}, bf16[2,3,48,512]{3,2,1,0:T(8,128)(2,1)S(1)}, u32[]{:S(2)}, u32[]{:S(2)}) collective-permute-start(bf16[2,3,48,512]{3,2,1,0:T(8,128)(2,1)S(1)} %slice.61), channel_id=1, source_target_pairs={{2,0},{4,2},{6,4},{0,6},{3,1},{5,3},{7,5},{1,7},{10,8},{12,10},{14... | collective-permute-start | bytes 884744 | tf_op jit(solution)/shard_map/ppermute | solution.py:45
  21.2 7.1 %collective-permute-start.2 = (bf16[3,48]{1,0:T(4,128)(2,1)S(1)}, bf16[3,48]{1,0:T(4,128)(2,1)S(1)}, u32[]{:S(2)}, u32[]{:S(2)}) collective-permute-start(bf16[3,48]{1,0:T(4,128)(2,1)S(1)} %slice.66), channel_id=1, source_target_pairs={{2,0},{4,2},{6,4},{0,6},{3,1},{5,3},{7,5},{1,7},{10,8},{12,10},{14... | collective-permute-start | bytes 872 | tf_op jit(solution)/shard_map/ppermute | solution.py:45
  21.7 319.2 %all-gather.8.cloned.1.call-start = ((), (), s32[]{:S(2)}) async-start(), calls=%async_computation.2 | async-start | bytes 2162688 | tf_op jit(solution)/shard_map/all_gather | solution.py:144
  28.3 3.7 %collective-permute-start.3 = (bf16[24,6]{1,0:T(8,128)(2,1)S(1)}, bf16[24,6]{1,0:T(8,128)(2,1)S(1)}, u32[]{:S(2)}, u32[]{:S(2)}) collective-permute-start(bf16[24,6]{1,0:T(8,128)(2,1)S(1)} %pad_maximum_fusion.9), channel_id=1, source_target_pairs={{1,0},{0,1},{3,2},{2,3},{5,4},{4,5},{7,6},{6,7},{9,8},{8,9},{11,10... | collective-permute-start | bytes 872 | tf_op jit(solution)/shard_map/ppermute | solution.py:45
  28.5 4.0 %collective-permute-start.5 = (bf16[2,512,16]{1,2,0:T(8,128)(2,1)S(1)}, bf16[2,512,16]{1,2,0:T(8,128)(2,1)S(1)}, u32[]{:S(2)}, u32[]{:S(2)}) collective-permute-start(bf16[2,512,16]{1,2,0:T(8,128)(2,1)S(1)} %pad_maximum_fusion.8), channel_id=1, source_target_pairs={{0,2},{1,3},{2,0},{3,1},{4,6},{5,7},{6,4},{7,5},{8,10},{9,11},{10,... | collective-permute-start | bytes 98312 | tf_op jit(solution)/shard_map/ppermute | solution.py:26
  32.6 5.2 %collective-permute-start.6 = (bf16[4,512,16]{1,2,0:T(8,128)(2,1)S(1)}, bf16[4,512,16]{1,2,0:T(8,128)(2,1)S(1)}, u32[]{:S(2)}, u32[]{:S(2)}) collective-permute-start(bf16[4,512,16]{1,2,0:T(8,128)(2,1)S(1)} %pad_maximum_fusion.7), channel_id=1, source_target_pairs={{0,4},{1,5},{2,6},{3,7},{4,0},{5,1},{6,2},{7,3},{8,12},{9,13},{10,... | collective-permute-start | bytes 196616 | tf_op jit(solution)/shard_map/ppermute | solution.py:26
  37.8 1.5 collective-permute-start.7
  39.4 9.4 %collective-permute-start.8 = (bf16[16,512,16]{1,2,0:T(8,128)(2,1)S(1)}, bf16[16,512,16]{1,2,0:T(8,128)(2,1)S(1)}, u32[]{:S(2)}, u32[]{:S(2)}) collective-permute-start(bf16[16,512,16]{1,2,0:T(8,128)(2,1)S(1)} %pad_maximum_fusion.5), channel_id=1, source_target_pairs={{0,16},{1,17},{2,18},{3,19},{4,20},{5,21},{6,22},{7,23},{8,24},{9,... | collective-permute-start | bytes 786440 | tf_op jit(solution)/shard_map/ppermute | solution.py:26
  41.0 11.5 %collective-permute-start.1 = (bf16[2,24,6,512]{3,2,1,0:T(8,128)(2,1)S(1)}, bf16[2,24,6,512]{3,2,1,0:T(8,128)(2,1)S(1)}, u32[]{:S(2)}, u32[]{:S(2)}) collective-permute-start(bf16[2,24,6,512]{3,2,1,0:T(8,128)(2,1)S(1)} %pad_maximum_fusion.3), channel_id=1, source_target_pairs={{1,0},{0,1},{3,2},{2,3},{5,4},{4,5},{7,6},{6,7},{9,8},{8,9},{11,10... | collective-permute-start | bytes 884744 | tf_op jit(solution)/shard_map/ppermute | solution.py:45
  264.6 11.4 %copy-start.4 = (bf16[2304,512]{1,0:T(8,128)(2,1)}, bf16[2304,512]{1,0:T(8,128)(2,1)S(1)}, u32[]{:S(2)}) copy-start(bf16[2304,512]{1,0:T(8,128)(2,1)S(1)} %convolution_convert_fusion.1) | copy-start | bytes 7077892
  264.6 21.6 %copy-start.1 = (bf16[1,2,24,48,512]{4,3,2,1,0:T(8,128)(2,1)S(1)}, bf16[1,2,24,48,512]{4,3,2,1,0:T(8,128)(2,1)}, u32[]{:S(2)}) copy-start(bf16[1,2,24,48,512]{4,3,2,1,0:T(8,128)(2,1)} %param.8) | copy-start | bytes 7077892
  264.7 11.3 %collective-permute-start.9 = (bf16[2,24,6,512]{3,2,1,0:T(8,128)(2,1)S(1)}, bf16[2,24,6,512]{3,2,1,0:T(8,128)(2,1)S(1)}, u32[]{:S(2)}, u32[]{:S(2)}) collective-permute-start(bf16[2,24,6,512]{3,2,1,0:T(8,128)(2,1)S(1)} %slice.71), channel_id=1, source_target_pairs={{1,0},{0,1},{3,2},{2,3},{5,4},{4,5},{7,6},{6,7},{9,8},{8,9},{11,10... | collective-permute-start | bytes 884744 | tf_op jit(solution)/shard_map/ppermute | solution.py:45
  276.1 10.1 %collective-permute-start.10 = (bf16[2,3,48,512]{3,2,1,0:T(8,128)(2,1)S(1)}, bf16[2,3,48,512]{3,2,1,0:T(8,128)(2,1)S(1)}, u32[]{:S(2)}, u32[]{:S(2)}) collective-permute-start(bf16[2,3,48,512]{3,2,1,0:T(8,128)(2,1)S(1)} %pad_maximum_fusion.4), channel_id=1, source_target_pairs={{6,0},{0,2},{2,4},{4,6},{7,1},{1,3},{3,5},{5,7},{14,8},{8,10},{10,... | collective-permute-start | bytes 884744 | tf_op jit(solution)/shard_map/ppermute | solution.py:45
  279.4 6.9 %copy-start.2 = (bf16[2,21,48,512]{3,2,1,0:T(8,128)(2,1)}, bf16[2,21,48,512]{3,2,1,0:T(8,128)(2,1)S(1)}, u32[]{:S(2)}) copy-start(bf16[2,21,48,512]{3,2,1,0:T(8,128)(2,1)S(1)} %pad_maximum_fusion.1) | copy-start | bytes 6193156
  291.7 2.3 copy-start.9
  341.0 8.5 %copy-start.3 = (bf16[2,21,48,512]{3,2,1,0:T(8,128)(2,1)S(1)}, bf16[2,21,48,512]{3,2,1,0:T(8,128)(2,1)}, u32[]{:S(2)}) copy-start(bf16[2,21,48,512]{3,2,1,0:T(8,128)(2,1)} %copy-done.2) | copy-start | bytes 6193156
Sparse Core Ops, SparseCore 0:
  10.3 60.1 all-gather.3
  73.5 55.2 all-gather.5
  276.7 56.4 all-gather.7
